TPU v7x, 32 devices: a whole 2x2x4 slice. The times are simulated.
32 devices in a mesh: expert: 2 (over y), shard: 16 (over z, x, core).
Axes of the slice: x: 2, y: 2, z: 4, core: 2. Of those that a mesh axis runs over, the one named last changes fastest.
Arguments:
- fast_weights: bfloat16 [2, 16, 1, 64, 14336], P('expert', 'shard'), may hold values from -0.125 to 0.125
- slow_weights: float32 [2, 1, 64, 14336], P('expert', None, None, 'shard'), may hold values from -0.09375 to 0.09375
- step_counts: int32 [2, 16], P('expert', 'shard'), may hold values from 1 to 16
- token_counts: int32 [2, 16], P('expert', 'shard'), may hold values from 100 to 897
Outputs:
- new_slow: float32 [2, 1, 64, 14336], P('expert', None, None, 'shard')
- reset_fast: bfloat16 [2, 1, 64, 14336], P('expert')
All inputs are finite; a program needn't handle non-finite values.
Results may differ from a plain program's by a relative error of at most 0.001.
Values may be sent and summed in bfloat16 or wider, within the bound.
A program may use at most 64 MiB of HBM per device.

v0:
```python
import jax
import jax.numpy as jnp
from jax import lax
from jax.sharding import PartitionSpec as P

outer_rate = 0.7


def shards(fast_weights, slow_weights, step_counts, token_counts):
    tokens = token_counts.astype(jnp.float32)[0, 0]
    steps = step_counts.astype(jnp.float32)[0, 0]
    share = tokens / steps
    work = tokens * steps
    groups = lax.axis_size("expert")
    tok_e, work_e, qsum = lax.psum((tokens, work, share), "shard")
    total = lax.psum(tok_e, "expert")
    rate = outer_rate * groups * work_e / (tok_e * total)
    weighted = share * fast_weights[0, 0].astype(jnp.float32)
    slow_part = slow_weights[0]
    mixed = lax.psum_scatter(weighted, "shard", scatter_dimension=2, tiled=True)
    new_slow = slow_part + rate * (mixed - qsum * slow_part)
    reset = lax.all_gather(new_slow.astype(jnp.bfloat16), "shard", axis=2, tiled=True)
    return (new_slow[None], reset[None])


def solution(mesh):
    placed = (
        P("expert", "shard", None, None, None),
        P("expert", None, None, "shard"),
        P("expert", "shard"),
        P("expert", "shard"),
    )
    return jax.shard_map(
        shards,
        mesh=mesh,
        in_specs=placed,
        out_specs=(P("expert", None, None, "shard"), P("expert", None, None, None)),
        check_vma=False,
    )
```

profile of v0, /device:TPU:0, one launch (start us, length us, event | category | flops | bytes accessed | tf_op | source)
XLA Modules:
  0.0 136.1 jit_solution(3174609490786188640)
XLA Ops:
  7.2 0.0 reduce-scatter.2.cloned.1.call-start
  8.5 0.0 copy-start
  8.6 3.6 %multiply_bitcast_fusion = f32[1,64,14336]{2,1,0:T(8,128)} fusion(bf16[1,1,1,64,14336]{4,3,2,1,0:T(8,128)(2,1)} %param.4, f32[]{:T(128)S(6)} %div.7), kind=kLoop, calls=%fused_computation | loop fusion | flops 1835008 | bytes 5505028 | tf_op jit(solution)/shard_map/mul | solution.py:18
  12.1 0.0 reduce-scatter.2.cloned.1.call-update
  12.2 0.0 all-gather.2.cloned.1.call-start
  12.2 36.3 %all-reduce = (f32[]{:T(128)}, f32[]{:T(128)}, f32[]{:T(128)}) all-reduce(f32[]{:T(128)S(6)} %div.7, f32[]{:T(128)S(6)} %mul.43, f32[]{:T(128)} %bitcast.1), channel_id=1, replica_groups=mesh['expert'=2,'shard'=16] {'shard'}, use_global_device_ids=true, to_apply=%region_4.0 | all-reduce | flops 3 | bytes 24 | tf_op jit(solution)/shard_map/psum | solution.py:15
  48.6 5.6 %psum.30 = f32[]{:T(128)} all-reduce(f32[]{:T(128)} %get-tuple-element.4), channel_id=1, replica_groups=mesh['expert'=2,'shard'=16] {'expert'}, use_global_device_ids=true, to_apply=%region_2.0 | all-reduce | flops 1 | bytes 8 | tf_op jit(solution)/shard_map/psum | solution.py:16
  56.1 27.5 %reduce-scatter.2.cloned.1.call-done = f32[1,64,896]{2,1,0:T(8,128)} async-done(((f32[1,64,14336]{2,1,0:T(8,128)}), f32[1,64,896]{2,1,0:T(8,128)}) %reduce-scatter.2.cloned.1.call-update) | async-done | bytes 229392 | tf_op jit(solution)/shard_map/reduce_scatter | solution.py:20
  83.6 0.0 copy-done
  83.6 2.4 %fusion.2 = (bf16[1,64,896]{2,1,0:T(8,128)(2,1)}, f32[1,1,64,896]{3,2,1,0:T(8,128)}) fusion(f32[1,64,896]{2,1,0:T(8,128)} %reduce-scatter.2.cloned.1.call-done, f32[]{:T(128)} %get-tuple-element.2, f32[]{:T(128)S(6)} %div.6, f32[1,1,64,896]{3,2,1,0:T(8,128)S(1)} %copy-done), kind=kLoop, calls=%fused_computation.5 | loop fusion | flops 286720 | bytes 802824 | tf_op jit(solution)/shard_map/convert_element_type | solution.py:22
  86.0 0.0 all-gather.2.cloned.1.call-update
  86.0 40.4 %all-gather.2.cloned.1.call-done = bf16[1,64,14336]{2,1,0:T(8,128)(2,1)} async-done(((bf16[1,64,896]{2,1,0:T(8,128)(2,1)}), bf16[1,64,14336]{2,1,0:T(8,128)(2,1)}) %all-gather.2.cloned.1.call-update) | async-done | bytes 1835024 | tf_op jit(solution)/shard_map/all_gather | solution.py:22
  126.4 2.8 %copy.9 = bf16[1,1,64,14336]{3,2,1,0:T(8,128)(2,1)} copy(bf16[1,1,64,14336]{3,2,1,0:T(8,128)(2,1)} %bitcast.20) | data formatting | bytes 3670016
Async XLA Ops:
  7.2 76.4 %reduce-scatter.2.cloned.1.call-start = ((), (), s32[]{:S(2)}) async-start(), calls=%async_computation.1 | async-start | bytes 3899392 | tf_op jit(solution)/shard_map/reduce_scatter | solution.py:20
  8.5 75.0 %copy-start = (f32[1,1,64,896]{3,2,1,0:T(8,128)S(1)}, f32[1,1,64,896]{3,2,1,0:T(8,128)}, u32[]{:S(2)}) copy-start(f32[1,1,64,896]{3,2,1,0:T(8,128)} %param.5) | copy-start | bytes 688132
  12.2 114.2 %all-gather.2.cloned.1.call-start = ((), (), s32[]{:S(2)}) async-start(), calls=%async_computation.2 | async-start | bytes 1949696 | tf_op jit(solution)/shard_map/all_gather | solution.py:22
Sparse Core Ops, SparseCore 0:
  12.3 71.2 reduce-scatter.1
  86.5 39.8 all-gather.1
where the time goes:
time: 136 us
  waiting for transfers between devices  67.9 us (50%)
  blocking collectives  41.9 us (31%)
  between operations  17.4 us (13%)
  other arithmetic  5.96 us (4%)
  local copies, waits for them, and re-layouts  2.85 us (2%)
    all_gather x1, waiting for transfers between devices, shards(): lax.all_gather(new_slow.astype(jnp.bfloat16), 'shard', axis=2, tiled=True)  40.4 us
    psum x1, blocking collectives, shards(): tok_e, work_e, qsum = lax.psum((tokens, work, share), 'shard')  36.3 us
    reduce_scatter x1, waiting for transfers between devices, shards(): mixed = lax.psum_scatter(weighted, 'shard', scatter_dimension=2, tiled=True)  27.5 us
    psum x1, blocking collectives, shards(): total = lax.psum(tok_e, 'expert')  5.57 us
    mul x1, other arithmetic, shards(): weighted = share * fast_weights[0, 0].astype(jnp.float32)  3.59 us
    unnamed x3, local copies, waits for them, and re-layouts  2.85 us
  transfers between devices with their start and end apart: 2, of which 2 were waited for; matrix products, arithmetic and copies ran while one was open for 0% of the time, Pallas kernels for 0%

commit v1 on v0

--- a/solution.py
+++ b/solution.py
@@ -1,12 +1,238 @@
+import functools
+
 import jax
 import jax.numpy as jnp
 from jax import lax
+from jax.experimental import pallas as pl
+from jax.experimental.pallas import tpu as pltpu
 from jax.sharding import PartitionSpec as P
 
 outer_rate = 0.7
-
-
-def shards(fast_weights, slow_weights, step_counts, token_counts):
+MESH = pl.DeviceIdType.MESH
+LANES = 128
+PLANE = 4
+
+
+def xor(inner, d):
+    hi, lo = inner // 2, inner % 2
+    return (hi + d // 2) % 2 * 2 + (lo + d % 2) % 2
+
+
+def order_of(z, length):
+    step = -1 if 2 * z < length - 1 else 1
+    ts = [t for t in range(length)[::step] if t != z]
+    return sorted(ts, key=lambda t: -abs(t - z))
+
+
+def kernel(groups, length, pieces, fast, slow, steps, tokens, new_ref, full_ref,
+           raw, left, right, outb, slow_v, stat, plane_stat, sems_s, sems_r, sem_l):
+    rows, width = slow.shape
+    part = rows // pieces
+    e = lax.axis_index("expert")
+    s = lax.axis_index("shard")
+    z, inner = s // PLANE, s % PLANE
+
+    def cols(t, i):
+        return pl.ds(pl.multiple_of((t * PLANE + i) * width, LANES), width)
+
+    def span(h):
+        return pl.ds(h * part, part)
+
+    barrier = pltpu.get_barrier_semaphore()
+    peers = [((e + k) % groups, z * PLANE + xor(inner, d)) for k in range(groups) for d in range(PLANE) if k or d]
+    peers += [(e, (z + k) % length * PLANE + inner) for k in range(1, length)]
+    for peer in peers:
+        pl.semaphore_signal(barrier, inc=1, device_id=peer, device_id_type=MESH)
+    load_slow = pltpu.make_async_copy(slow, slow_v, sem_l.at[length])
+    load_slow.start()
+    own = [pltpu.make_async_copy(fast.at[:, cols(t, inner)], raw.at[0, t], sem_l.at[t]) for t in range(length)]
+    for copy in own:
+        copy.start()
+    stat[0, 0:8, :] = jnp.full((8, LANES), tokens[0, 0].astype(jnp.float32))
+    stat[0, 8:16, :] = jnp.full((8, LANES), steps[0, 0].astype(jnp.float32))
+    pl.semaphore_wait(barrier, len(peers))
+
+    def body(me):
+        count = [0]
+        sent = []
+
+        def push(src, dst, recv, peer):
+            copy = pltpu.make_async_remote_copy(
+                src_ref=src, dst_ref=dst, send_sem=sems_s.at[count[0]], recv_sem=sems_r.at[recv],
+                device_id=peer, device_id_type=MESH)
+            count[0] += 1
+            copy.start()
+            sent.append(copy)
+
+        def arrived(dst, recv):
+            pltpu.make_async_remote_copy(
+                src_ref=dst, dst_ref=dst, send_sem=sems_s.at[0], recv_sem=sems_r.at[recv],
+                device_id=(e, s), device_id_type=MESH).wait_recv()
+
+        base = 0
+        r_raw = lambda d, t, h: ((d - 1) * length + t) * pieces + h
+        base += (PLANE - 1) * length * pieces
+        r_left = lambda t, h, b=base: b + t * pieces + h
+        base += length * pieces
+        r_right = lambda t, h, b=base: b + t * pieces + h
+        base += length * pieces
+        r_z = lambda t, h, b=base: b + t * pieces + h
+        base += length * pieces
+        r_x = lambda t, h, b=base: b + t * pieces + h
+        base += length * pieces
+        r_sib = lambda t, x, h, b=base: b + (t * 2 + x) * pieces + h
+        base += 2 * length * pieces
+        r_stat = lambda i, b=base: b + i
+        base += groups * PLANE
+        r_plane = lambda k, b=base: b + k
+
+        at = lambda t, i: (e, t * PLANE + i)
+        far = order_of(me, length)
+        items = []
+        for h in range(pieces):
+            items += [(h, t) for t in far[:1]]
+            if h:
+                items.append((h - 1, me))
+            items += [(h, t) for t in far[1:]]
+        items.append((pieces - 1, me))
+
+        for k in range(groups):
+            for d in range(PLANE):
+                if k or d:
+                    i = (groups - k) % groups * PLANE + d
+                    push(stat.at[0], stat.at[i], r_stat(i), ((e + k) % groups, me * PLANE + xor(inner, d)))
+        for h, t in items:
+            for d in (2, 3, 1):
+                push(fast.at[span(h), cols(t, xor(inner, d))], raw.at[d, t, span(h)], r_raw(d, t, h), at(me, xor(inner, d)))
+
+        def stats_in():
+            for i in range(1, groups * PLANE):
+                arrived(stat.at[i], r_stat(i))
+            tok = [stat[i, 0:8, :] for i in range(groups * PLANE)]
+            stp = [stat[i, 8:16, :] for i in range(groups * PLANE)]
+            shares = [tok[i] / stp[i] for i in range(PLANE)]
+            plane_stat[0, 0:8, :] = sum(tok[:PLANE])
+            plane_stat[0, 8:16, :] = sum(tok[i] * stp[i] for i in range(PLANE))
+            plane_stat[0, 16:24, :] = sum(shares)
+            plane_stat[0, 24:32, :] = sum(tok)
+            return [v[0:1, 0:1] for v in shares]
+
+        shares = stats_in()
+        for copy in own:
+            copy.wait()
+
+        def finish(h, first):
+            if first:
+                load_slow.wait()
+                for k in range(1, length):
+                    arrived(plane_stat.at[k], r_plane(k))
+            tok, work, qsum, total = (
+                sum(plane_stat[k, 8 * j:8 * j + 8, :] for k in range(length))[0:1, 0:1] for j in range(4))
+            rate = outer_rate * groups * work / (tok * total)
+            return rate, qsum
+
+        def spread(t, h):
+            ref = full_ref.at[span(h), cols(t, inner)]
+            push(ref, ref, r_x(t, h), at(me, xor(inner, 2)))
+            push(ref, ref, r_sib(t, 0, h), at(me, xor(inner, 1)))
+
+        def from_z(h):
+            for t in sorted((t for t in range(length) if t != me), key=lambda t: abs(t - me)):
+                arrived(full_ref.at[span(h), cols(t, inner)], r_z(t, h))
+                spread(t, h)
+
+        def from_x(h):
+            for t in sorted(range(length), key=lambda t: abs(t - me)):
+                i = xor(inner, 2)
+                ref = full_ref.at[span(h), cols(t, i)]
+                arrived(ref, r_x(t, h))
+                push(ref, ref, r_sib(t, 1, h), at(me, xor(inner, 1)))
+
+        for n, (h, t) in enumerate(items):
+            for d in range(1, PLANE):
+                arrived(raw.at[d, t, span(h)], r_raw(d, t, h))
+            came = []
+            if t >= me and me > 0:
+                arrived(left.at[t, span(h)], r_left(t, h))
+                came.append(left)
+            if t <= me and me < length - 1:
+                arrived(right.at[t, span(h)], r_right(t, h))
+                came.append(right)
+            if t == me:
+                rate, qsum = finish(h, h == 0)
+            for r0 in range(h * part, (h + 1) * part, 16):
+                sl = pl.ds(r0, 16)
+                acc = shares[0] * raw[0, t, sl, :].astype(jnp.float32)
+                for d in range(1, PLANE):
+                    acc += shares[d] * raw[d, t, sl, :].astype(jnp.float32)
+                for ref in came:
+                    acc += ref[t, sl, :]
+                if t == me:
+                    old = slow_v[sl, :]
+                    new = old + rate * (acc - qsum * old)
+                    new_ref[sl, :] = new
+                    full_ref[sl, cols(me, inner)] = new.astype(jnp.bfloat16)
+                else:
+                    outb[t, sl, :] = acc
+            if t == me:
+                ref = full_ref.at[span(h), cols(me, inner)]
+                for other in order_of(me, length):
+                    push(ref, ref, r_z(me, h), at(other, inner))
+                spread(me, h)
+            elif t > me:
+                push(outb.at[t, span(h)], left.at[t, span(h)], r_left(t, h), at(me + 1, inner))
+            else:
+                push(outb.at[t, span(h)], right.at[t, span(h)], r_right(t, h), at(me - 1, inner))
+            if n == 0:
+                for k in range(1, length):
+                    j = length - k
+                    push(plane_stat.at[0], plane_stat.at[j], r_plane(j), at((me + k) % length, inner))
+            if n == len(items) - 2:
+                for g in range(pieces - 1):
+                    from_z(g)
+        from_z(pieces - 1)
+        for h in range(pieces):
+            from_x(h)
+        for h in range(pieces):
+            for t in range(length):
+                arrived(full_ref.at[span(h), cols(t, xor(inner, 1))], r_sib(t, 0, h))
+                arrived(full_ref.at[span(h), cols(t, xor(inner, 3))], r_sib(t, 1, h))
+        for copy in sent:
+            copy.wait_send()
+
+    for me in range(length):
+        pl.when(z == me)(functools.partial(body, me))
+
+
+def shards_kernel(groups, devices, fast_weights, slow_weights, step_counts, token_counts):
+    rows, full = fast_weights.shape[-2:]
+    width = slow_weights.shape[-1]
+    length = devices // PLANE
+    pieces = 2
+    sems = length * pieces * (PLANE - 1 + 6) + groups * PLANE + length + 8
+    new, reset = pl.pallas_call(
+        functools.partial(kernel, groups, length, pieces),
+        out_shape=(jax.ShapeDtypeStruct((rows, width), jnp.float32), jax.ShapeDtypeStruct((rows, full), jnp.bfloat16)),
+        in_specs=[pl.BlockSpec(memory_space=pl.ANY)] * 2 + [pl.BlockSpec(memory_space=pltpu.SMEM)] * 2,
+        out_specs=(pl.BlockSpec(memory_space=pltpu.VMEM),) * 2,
+        scratch_shapes=[
+            pltpu.VMEM((PLANE, length, rows, width), jnp.bfloat16),
+            pltpu.VMEM((length, rows, width), jnp.float32),
+            pltpu.VMEM((length, rows, width), jnp.float32),
+            pltpu.VMEM((length, rows, width), jnp.float32),
+            pltpu.VMEM((rows, width), jnp.float32),
+            pltpu.VMEM((groups * PLANE, 16, LANES), jnp.float32),
+            pltpu.VMEM((length, 32, LANES), jnp.float32),
+            pltpu.SemaphoreType.DMA((sems,)),
+            pltpu.SemaphoreType.DMA((sems,)),
+            pltpu.SemaphoreType.DMA((length + 1,)),
+        ],
+        compiler_params=pltpu.CompilerParams(collective_id=0, has_side_effects=True),
+    )(fast_weights[0, 0, 0], slow_weights[0, 0], step_counts, token_counts)
+    return new[None, None], reset[None, None]
+
+
+def shards_plain(fast_weights, slow_weights, step_counts, token_counts):
     tokens = token_counts.astype(jnp.float32)[0, 0]
     steps = step_counts.astype(jnp.float32)[0, 0]
     share = tokens / steps
@@ -24,6 +250,15 @@
 
 
 def solution(mesh):
+    groups, devices = mesh.shape["expert"], mesh.shape["shard"]
+
+    def step(fast_weights, slow_weights, step_counts, token_counts):
+        layers, rows, width = slow_weights.shape[1:]
+        whole = devices % PLANE == 0 and devices > PLANE and rows % 32 == 0 and width % LANES == 0
+        if whole and layers == 1:
+            return shards_kernel(groups, devices, fast_weights, slow_weights, step_counts, token_counts)
+        return shards_plain(fast_weights, slow_weights, step_counts, token_counts)
+
     placed = (
         P("expert", "shard", None, None, None),
         P("expert", None, None, "shard"),
@@ -31,7 +266,7 @@
         P("expert", "shard"),
     )
     return jax.shard_map(
-        shards,
+        step,
         mesh=mesh,
         in_specs=placed,
         out_specs=(P("expert", None, None, "shard"), P("expert", None, None, None)),

time: 136 us -> 55.6 us (0.41)
  waiting for transfers between devices: 67.9 us -> 0 us
  Pallas kernels: 0 us -> 49 us
  blocking collectives: 41.9 us -> 0 us
  between operations: 17.4 us -> 1.93 us
  other arithmetic: 5.96 us -> 0 us
  local copies, waits for them, and re-layouts: 2.85 us -> 4.49 us
    pallas_call x0 -> x1, Pallas kernels: none -> 49 us  [shards_kernel(): pl.pallas_call(functools.partial(kernel, groups, length, pieces), out_sha...]
    psum x2 -> x0, blocking collectives: 41.9 us -> none  [the longest x1 36.3 us: shards(): tok_e, work_e, qsum = lax.psum((tokens, work, share), 'shard')]
    all_gather x1 -> x0, waiting for transfers between devices: 40.4 us -> none  [shards(): lax.all_gather(new_slow.astype(jnp.bfloat16), 'shard', axis=2, tiled=True)]
    reduce_scatter x1 -> x0, waiting for transfers between devices: 27.5 us -> none  [shards(): mixed = lax.psum_scatter(weighted, 'shard', scatter_dimension=2, tiled=True)]
    mul x1 -> x0, other arithmetic: 3.59 us -> none  [shards(): weighted = share * fast_weights[0, 0].astype(jnp.float32)]
    convert_element_type x1 -> x0, other arithmetic: 2.38 us -> none  [shards(): new_slow.astype(jnp.bfloat16)]
    unnamed x3 -> x2, local copies, waits for them, and re-layouts: 2.85 us -> 4.49 us
  transfers between devices with their start and end apart: 2 -> 0, of which waited for: 2 -> 0; matrix products, arithmetic and copies ran while one was open for 0% -> 0% of each run, Pallas kernels for 0% -> 0%
where the time goes in v1:
time: 55.6 us; the launch traced here: 55.4 us
  Pallas kernels  49 us (88%)
  local copies, waits for them, and re-layouts  4.49 us (8%)
  between operations  1.93 us (3%)
    pallas_call x1, Pallas kernels, shards_kernel(): pl.pallas_call(functools.partial(kernel, groups, length, pieces), out_sha...  49 us
    unnamed x2, local copies, waits for them, and re-layouts  4.49 us

profile of v1, /device:TPU:0, one launch (start us, length us, event | category | flops | bytes accessed | tf_op | source)
XLA Modules:
  0.0 55.4 jit_solution(18019566753814193287)
XLA Ops:
  1.9 49.0 %shard_map.59 = (f32[64,896]{1,0:T(8,128)}, bf16[64,14336]{1,0:T(8,128)(2,1)}) custom-call(bf16[64,14336]{1,0:T(8,128)(2,1)} %bitcast.4, f32[64,896]{1,0:T(8,128)} %bitcast.6, s32[1,1]{1,0:T(1,128)S(6)} %copy.8.steps, s32[1,1]{1,0:T(1,128)S(6)} %copy.9.tokens), custom_call_target="tpu_custom_call" | custom-call | tf_op jit(solution)/shard_map/pallas_call | solution.py:213
  50.9 1.6 %copy.10 = f32[1,1,64,896]{3,2,1,0:T(8,128)} copy(f32[1,1,64,896]{3,2,1,0:T(8,128)} %bitcast.7) | data formatting | bytes 458752
  52.5 2.8 %copy.11 = bf16[1,1,64,14336]{3,2,1,0:T(8,128)(2,1)} copy(bf16[1,1,64,14336]{3,2,1,0:T(8,128)(2,1)} %bitcast.5) | data formatting | bytes 3670016

commit v2 on v1

--- a/solution.py
+++ b/solution.py
@@ -24,10 +24,29 @@
     return sorted(ts, key=lambda t: -abs(t - z))
 
 
-def kernel(groups, length, pieces, fast, slow, steps, tokens, new_ref, full_ref,
+def PLAN(far, me, pieces, lag=4, zlag=8):
+    plan, owned, passed = [], 0, 0
+    sums = [(h, t) for h in range(pieces) for t in far]
+    for n in range(len(sums) + max(lag, zlag) + 1):
+        if owned < pieces and n >= (owned + 1) * len(far) + lag or (n >= len(sums) and owned < pieces):
+            plan.append(("r", owned, me))
+            owned += 1
+        if passed < owned and n >= (passed + 1) * len(far) + zlag:
+            plan.append(("z", passed, me))
+            passed += 1
+        if n < len(sums):
+            plan.append(("r", *sums[n]))
+    plan += [("r", h, me) for h in range(owned, pieces)]
+    plan += [("z", h, me) for h in range(passed, pieces)]
+    plan += [("x", h, me) for h in range(pieces)]
+    feed = [(h, t) for what, h, t in plan if what == "r"]
+    return feed, plan
+
+
+def kernel(groups, length, bounds, fast, slow, steps, tokens, new_ref, full_ref,
            raw, left, right, outb, slow_v, stat, plane_stat, sems_s, sems_r, sem_l):
     rows, width = slow.shape
-    part = rows // pieces
+    pieces = len(bounds) - 1
     e = lax.axis_index("expert")
     s = lax.axis_index("shard")
     z, inner = s // PLANE, s % PLANE
@@ -36,7 +55,7 @@
         return pl.ds(pl.multiple_of((t * PLANE + i) * width, LANES), width)
 
     def span(h):
-        return pl.ds(h * part, part)
+        return pl.ds(bounds[h], bounds[h + 1] - bounds[h])
 
     barrier = pltpu.get_barrier_semaphore()
     peers = [((e + k) % groups, z * PLANE + xor(inner, d)) for k in range(groups) for d in range(PLANE) if k or d]
@@ -88,22 +107,21 @@
 
         at = lambda t, i: (e, t * PLANE + i)
         far = order_of(me, length)
-        items = []
-        for h in range(pieces):
-            items += [(h, t) for t in far[:1]]
-            if h:
-                items.append((h - 1, me))
-            items += [(h, t) for t in far[1:]]
-        items.append((pieces - 1, me))
+        feed, plan = PLAN(far, me, pieces)
 
         for k in range(groups):
             for d in range(PLANE):
                 if k or d:
                     i = (groups - k) % groups * PLANE + d
                     push(stat.at[0], stat.at[i], r_stat(i), ((e + k) % groups, me * PLANE + xor(inner, d)))
-        for h, t in items:
+        def give(n):
+            h, t = feed[n]
             for d in (2, 3, 1):
                 push(fast.at[span(h), cols(t, xor(inner, d))], raw.at[d, t, span(h)], r_raw(d, t, h), at(me, xor(inner, d)))
+
+        for n in range(min(8, len(feed))):
+            give(n)
+        given = [min(8, len(feed))]
 
         def stats_in():
             for i in range(1, groups * PLANE):
@@ -148,9 +166,18 @@
                 arrived(ref, r_x(t, h))
                 push(ref, ref, r_sib(t, 1, h), at(me, xor(inner, 1)))
 
-        for n, (h, t) in enumerate(items):
+        for n, (what, h, t) in enumerate(plan):
+            if what == "z":
+                from_z(h)
+                continue
+            if what == "x":
+                from_x(h)
+                continue
             for d in range(1, PLANE):
                 arrived(raw.at[d, t, span(h)], r_raw(d, t, h))
+            if given[0] < len(feed):
+                give(given[0])
+                given[0] += 1
             came = []
             if t >= me and me > 0:
                 arrived(left.at[t, span(h)], r_left(t, h))
@@ -160,7 +187,7 @@
                 came.append(right)
             if t == me:
                 rate, qsum = finish(h, h == 0)
-            for r0 in range(h * part, (h + 1) * part, 16):
+            for r0 in range(bounds[h], bounds[h + 1], 16):
                 sl = pl.ds(r0, 16)
                 acc = shares[0] * raw[0, t, sl, :].astype(jnp.float32)
                 for d in range(1, PLANE):
@@ -187,12 +214,6 @@
                 for k in range(1, length):
                     j = length - k
                     push(plane_stat.at[0], plane_stat.at[j], r_plane(j), at((me + k) % length, inner))
-            if n == len(items) - 2:
-                for g in range(pieces - 1):
-                    from_z(g)
-        from_z(pieces - 1)
-        for h in range(pieces):
-            from_x(h)
         for h in range(pieces):
             for t in range(length):
                 arrived(full_ref.at[span(h), cols(t, xor(inner, 1))], r_sib(t, 0, h))
@@ -208,11 +229,12 @@
     rows, full = fast_weights.shape[-2:]
     width = slow_weights.shape[-1]
     length = devices // PLANE
-    pieces = 2
+    bounds = tuple(range(0, rows + 1, max(rows // 64, 1) * 16))
+    pieces = len(bounds) - 1
     sems = length * pieces * (PLANE - 1 + 6) + groups * PLANE + length + 8
     new, reset = pl.pallas_call(
-        functools.partial(kernel, groups, length, pieces),
-        out_shape=(jax.ShapeDtypeStruct((rows, width), jnp.float32), jax.ShapeDtypeStruct((rows, full), jnp.bfloat16)),
+        functools.partial(kernel, groups, length, bounds),
+        out_shape=(pltpu.VMEM((rows, width), jnp.float32), pltpu.VMEM((rows, full), jnp.bfloat16)),
         in_specs=[pl.BlockSpec(memory_space=pl.ANY)] * 2 + [pl.BlockSpec(memory_space=pltpu.SMEM)] * 2,
         out_specs=(pl.BlockSpec(memory_space=pltpu.VMEM),) * 2,
         scratch_shapes=[
@@ -254,7 +276,7 @@
 
     def step(fast_weights, slow_weights, step_counts, token_counts):
         layers, rows, width = slow_weights.shape[1:]
-        whole = devices % PLANE == 0 and devices > PLANE and rows % 32 == 0 and width % LANES == 0
+        whole = devices % PLANE == 0 and devices > PLANE and rows % 64 == 0 and width % LANES == 0
         if whole and layers == 1:
             return shards_kernel(groups, devices, fast_weights, slow_weights, step_counts, token_counts)
         return shards_plain(fast_weights, slow_weights, step_counts, token_counts)

time: 55.6 us -> 49.7 us (0.89)
  Pallas kernels: 49 us -> 45.6 us
  local copies, waits for them, and re-layouts: 4.49 us -> 1.92 us
    pallas_call x1, Pallas kernels: 49 us -> 45.6 us  [shards_kernel(): pl.pallas_call(functools.partial(kernel, groups, length, bounds), out_sha...]
    unnamed x2, local copies, waits for them, and re-layouts: 4.49 us -> 1.92 us
where the time goes in v2:
time: 49.7 us; the launch traced here: 49.4 us
  Pallas kernels  45.6 us (92%)
  between operations  1.93 us (4%)
  local copies, waits for them, and re-layouts  1.92 us (4%)
    pallas_call x1, Pallas kernels, shards_kernel(): pl.pallas_call(functools.partial(kernel, groups, length, bounds), out_sha...  45.6 us
    unnamed x2, local copies, waits for them, and re-layouts  1.92 us

profile of v2, /device:TPU:0, one launch (start us, length us, event | category | flops | bytes accessed | tf_op | source)
XLA Modules:
  0.0 49.4 jit_solution(13322510677189411749)
XLA Ops:
  1.9 45.6 %shard_map.59 = (f32[64,896]{1,0:T(8,128)S(1)}, bf16[64,14336]{1,0:T(8,128)(2,1)S(1)}) custom-call(bf16[64,14336]{1,0:T(8,128)(2,1)} %bitcast.6, f32[64,896]{1,0:T(8,128)} %bitcast.7, s32[1,1]{1,0:T(1,128)S(6)} %copy.10.steps, s32[1,1]{1,0:T(1,128)S(6)} %copy.11.tokens), custom_call_target="tpu_custom_call" | custom-call | tf_op jit(solution)/shard_map/pallas_call | solution.py:235
  47.5 0.7 %copy.8 = f32[1,1,64,896]{3,2,1,0:T(8,128)} copy(f32[1,1,64,896]{3,2,1,0:T(8,128)S(1)} %bitcast.5) | data formatting | bytes 458752
  48.2 1.2 %copy.9 = bf16[1,1,64,14336]{3,2,1,0:T(8,128)(2,1)} copy(bf16[1,1,64,14336]{3,2,1,0:T(8,128)(2,1)S(1)} %bitcast.4) | data formatting | bytes 3670016
